TPU v7x, 32 devices: a whole 2x2x4 slice. The times are simulated.
32 devices in a mesh: dp: 16 (over z, x, core), mp: 2 (over y).
Axes of the slice: x: 2, y: 2, z: 4, core: 2. Of those that a mesh axis runs over, the one named last changes fastest.
Arguments:
- node_feats: bfloat16 [256, 32768], P('mp', 'dp'), may hold values from -6 to 6
- proj_weight: bfloat16 [256, 256], P('mp'), may hold values from -0.375 to 0.375
- att_src: float32 [256], P('mp'), may hold values from -32 to 32
- att_dst: float32 [256], P('mp'), may hold values from -32 to 32
- out_bias: float32 [256], P('mp'), may hold values from -3 to 3
- tile_rows: int32 [512], P('dp'), may hold values from 0 to 255, as said below
- tile_cols: int32 [512], P('dp'), may hold values from 0 to 255, as said below
- tile_masks: int32 [512, 4, 128], P('dp'), may hold values from -2147483648 to 2147483646
Outputs:
- node_out: bfloat16 [256, 32768], P('mp', 'dp')
Inputs may be any that keep to these rules, and one draw needn't show every extreme that they name: `tile_rows`: block b holds nodes 128 b to 128 b + 127 and belongs to index b // 16 of dp. Among the 32 tiles of one index of dp, no owner's blocks are named more than 4 times; on every index one owner's blocks are named exactly 4 times. `tile_cols`: the same bound holds for source blocks: among the 32 tiles of one index of dp, no owner's blocks are named more than 4 times, and one owner's exactly 4 times on every index.
All inputs are finite; a program needn't handle non-finite values.
Results may differ from a plain program's by a relative error of at most 0.0034.
Values may be sent and summed in bfloat16 or wider, within the bound.
No kernel may reach another device: no remote copies, remote signals or barrier semaphores. Data moves between devices by JAX's collectives and lax.ppermute only.
A program may use at most 64 MiB of HBM per device.

v0:
```python
import math
import jax
import jax.numpy as jnp
from jax import lax
from jax.sharding import PartitionSpec as P

HD = 32
far_below = -1e30


def leaky_relu(scores):
    return jnp.where(scores > 0, scores, 0.2 * scores)


def unpack_bits(packed):
    offsets = jnp.arange(32, dtype=jnp.int32)
    spread = jnp.bitwise_and(jnp.right_shift(packed[..., :, None, :], offsets[:, None]), 1)
    return spread.reshape(packed.shape[:-2] + (packed.shape[-2] * 32, packed.shape[-1]))


def edge_scores(edge_mask, source, target):
    raw_scores = leaky_relu(target[:, :, None, :] + source[:, :, :, None])
    return jnp.where(edge_mask[:, None] == 1, raw_scores, far_below)


def tile_group(inputs):
    packed, feats_here, source_here, target_here = inputs
    edge_mask = unpack_bits(packed)
    scores = edge_scores(edge_mask, source_here, target_here)
    tile_peaks = jnp.max(scores, axis=2)
    weights = jnp.where(edge_mask[:, None] == 1, jnp.exp(scores - tile_peaks[:, :, None, :]), 0.0)
    masses = jnp.sum(weights, axis=2)
    values = jnp.einsum(
        "ghdc,ghcr->ghdr",
        feats_here,
        weights.astype(jnp.bfloat16),
        preferred_element_type=jnp.float32,
    )
    return (tile_peaks, masses, values)


def local(node_feats, proj_weight, att_src, att_dst, out_bias, tile_rows, tile_cols, tile_masks):
    local_rows = node_feats.shape[1]
    head_dims = proj_weight.shape[0]
    local_heads = head_dims // HD
    tile_size = tile_masks.shape[2]
    local_blocks = local_rows // tile_size
    tile_count = tile_rows.shape[0]
    devices_dp = lax.axis_size("dp")
    capacity = max(2, 2 * tile_count // devices_dp)
    slot_count = devices_dp * capacity
    projected = jnp.dot(
        proj_weight,
        lax.all_gather(node_feats, "mp", axis=0, tiled=True),
        preferred_element_type=jnp.float32,
    )
    features = projected.astype(jnp.bfloat16)
    by_head = projected.reshape(local_heads, HD, local_rows)
    source = jnp.einsum(
        "hd,hdn->hn", att_src.reshape(local_heads, HD), by_head, precision=lax.Precision.HIGHEST
    )
    target = jnp.einsum(
        "hd,hdn->hn", att_dst.reshape(local_heads, HD), by_head, precision=lax.Precision.HIGHEST
    )
    source_blocks = source.reshape(local_heads, local_blocks, tile_size).transpose(1, 0, 2)
    target_blocks = target.reshape(local_heads, local_blocks, tile_size).transpose(1, 0, 2)
    feat_blocks = features.reshape(local_heads, HD, local_blocks, tile_size).transpose(2, 0, 1, 3)

    def slots_of(block_ids):
        owners = block_ids // local_blocks
        position = jnp.arange(tile_count, dtype=jnp.int32)
        earlier = (owners[:, None] == owners[None, :]) & (position[None, :] < position[:, None])
        return (owners * capacity + jnp.sum(earlier, axis=1), block_ids % local_blocks)

    def to_slots(slot_ids, entries):
        slot_hits = slot_ids[:, None] == jnp.arange(slot_count, dtype=jnp.int32)[None, :]
        return jnp.sum(jnp.where(slot_hits, entries[:, None], 0), axis=0).reshape(
            devices_dp, capacity
        )

    col_slot, col_local = slots_of(tile_cols)
    row_slot, row_local = slots_of(tile_rows)
    col_wanted = to_slots(col_slot, col_local)
    wanted, wanted_rows = (
        lax.all_to_all(col_wanted, "dp", split_axis=0, concat_axis=0, tiled=True),
        lax.all_to_all(
            to_slots(row_slot, row_local), "dp", split_axis=0, concat_axis=0, tiled=True
        ),
    )
    send_source = jnp.take(source_blocks, wanted.reshape(-1), axis=0).reshape(
        devices_dp, capacity, local_heads, tile_size
    )
    send_target = jnp.take(target_blocks, wanted_rows.reshape(-1), axis=0).reshape(
        devices_dp, capacity, local_heads, tile_size
    )
    got_source, got_target = (
        lax.all_to_all(send_source, "dp", split_axis=0, concat_axis=0, tiled=True),
        lax.all_to_all(send_target, "dp", split_axis=0, concat_axis=0, tiled=True),
    )
    tile_source = jnp.take(got_source.reshape(slot_count, local_heads, tile_size), col_slot, axis=0)
    tile_target = jnp.take(got_target.reshape(slot_count, local_heads, tile_size), row_slot, axis=0)
    send_feats = jnp.take(feat_blocks, wanted.reshape(-1), axis=0).reshape(
        devices_dp, capacity, local_heads, HD, tile_size
    )
    got_feats = lax.all_to_all(send_feats, "dp", split_axis=0, concat_axis=0, tiled=True)
    tile_feats = jnp.take(
        got_feats.reshape(slot_count, local_heads, HD, tile_size), col_slot, axis=0
    )
    group_size = math.gcd(tile_count, 8)

    def grouped(stacked):
        return stacked.reshape((tile_count // group_size, group_size) + stacked.shape[1:])

    tile_peaks, masses, values = lax.map(
        tile_group,
        (grouped(tile_masks), grouped(tile_feats), grouped(tile_source), grouped(tile_target)),
    )
    tile_peaks = tile_peaks.reshape(tile_count, local_heads, tile_size)
    masses = masses.reshape(tile_count, local_heads, tile_size)
    values = values.reshape(tile_count, local_heads, HD, tile_size)
    slot_hits = row_slot[:, None] == jnp.arange(slot_count, dtype=jnp.int32)[None, :]
    filled = jnp.any(slot_hits, axis=0)
    source_tile = jnp.sum(
        jnp.where(slot_hits, jnp.arange(tile_count, dtype=jnp.int32)[:, None], 0), axis=0
    )
    send_values = jnp.where(
        filled[:, None, None, None], jnp.take(values, source_tile, axis=0), 0.0
    ).reshape(devices_dp, capacity, local_heads, HD, tile_size)
    send_peaks = jnp.where(
        filled[:, None, None], jnp.take(tile_peaks, source_tile, axis=0), far_below
    ).reshape(devices_dp, capacity, local_heads, tile_size)
    send_masses = jnp.where(
        filled[:, None, None], jnp.take(masses, source_tile, axis=0), 0.0
    ).reshape(devices_dp, capacity, local_heads, tile_size)
    send_codes = (
        jnp.where(filled, jnp.take(row_local, source_tile), 0)
        .astype(jnp.float32)
        .reshape(devices_dp, capacity)
    )
    got_values, got_peaks, got_masses, got_codes = (
        lax.all_to_all(send_values, "dp", split_axis=0, concat_axis=0, tiled=True),
        lax.all_to_all(send_peaks, "dp", split_axis=0, concat_axis=0, tiled=True),
        lax.all_to_all(send_masses, "dp", split_axis=0, concat_axis=0, tiled=True),
        lax.all_to_all(send_codes, "dp", split_axis=0, concat_axis=0, tiled=True),
    )
    got_values = got_values.reshape(slot_count, local_heads, HD, tile_size)
    got_peaks = got_peaks.reshape(slot_count, local_heads, tile_size)
    got_masses = got_masses.reshape(slot_count, local_heads, tile_size)
    row_codes = got_codes.reshape(slot_count).astype(jnp.int32)
    self_scores = leaky_relu(source_blocks + target_blocks)
    row_peak = self_scores.at[row_codes].max(got_peaks)
    rescale = jnp.exp(got_peaks - row_peak[row_codes])
    self_weight = jnp.exp(self_scores - row_peak)
    denominator = self_weight.at[row_codes].add(rescale * got_masses)
    summed = (
        (self_weight[:, :, None, :] * feat_blocks.astype(jnp.float32))
        .at[row_codes]
        .add(rescale[:, :, None, :] * got_values)
    )
    gathered = summed / denominator[:, :, None, :]
    flat_out = gathered.transpose(1, 2, 0, 3).reshape(head_dims, local_rows)
    return jax.nn.elu(flat_out + node_feats.astype(jnp.float32) + out_bias[:, None]).astype(
        jnp.bfloat16
    )


def solution(mesh):
    return jax.shard_map(
        local,
        mesh=mesh,
        in_specs=(
            P("mp", "dp"),
            P("mp", None),
            P("mp"),
            P("mp"),
            P("mp"),
            P("dp"),
            P("dp"),
            P("dp", None, None),
        ),
        out_specs=P("mp", "dp"),
        check_vma=False,
    )
```

profile of v0, /device:TPU:11, one launch (start us, length us, event | category | flops | bytes accessed | tf_op | source)
XLA Modules:
  0.0 289.5 jit_solution(12951224629687775602)
XLA Ops:
  9.4 6.5 %all-to-all-start.1 = ((s32[16,1,4]{2,1,0:T(1,128)}), s32[16,1,4]{2,1,0:T(1,128)S(1)}, u32[]{:S(2)}, u32[]{:S(2)}) async-start(s32[16,1,4]{2,1,0:T(1,128)} %bitcast.21), calls=%async_computation.1 | async-start | bytes 16384 | tf_op jit(solution)/shard_map/all_to_all | solution.py:86
  17.4 0.7 reshape.465
  18.2 0.7 reshape.467
  19.8 6.0 %all-to-all-start.3 = ((s32[16,1,4]{2,1,0:T(1,128)}), s32[16,1,4]{2,1,0:T(1,128)S(1)}, u32[]{:S(2)}, u32[]{:S(2)}) async-start(s32[16,1,4]{2,1,0:T(1,128)} %bitcast.27), calls=%async_computation.3 | async-start | bytes 16384 | tf_op jit(solution)/shard_map/all_to_all | solution.py:85
  27.0 2.7 all-to-all-done.3
  31.4 1.5 fusion.30
  34.4 0.8 broadcast_select_fusion.3
  35.2 6.2 %all-to-all-start.2 = ((f32[16,4,4,128]{3,2,1,0:T(4,128)}), f32[16,4,4,128]{3,2,1,0:T(4,128)S(1)}, u32[]{:S(2)}, u32[]{:S(2)}) async-start(f32[16,4,4,128]{3,2,1,0:T(4,128)} %bitcast.24), calls=%async_computation.2 | async-start | bytes 262144 | tf_op jit(solution)/shard_map/all_to_all | solution.py:98
  43.1 1.0 gather_fusion.1
  44.0 1.4 broadcast_select_fusion.2
  45.5 1.1 all-to-all-done.2
  46.6 6.2 %all-to-all-start.4 = ((f32[16,4,4,128]{3,2,1,0:T(4,128)}), f32[16,4,4,128]{3,2,1,0:T(4,128)S(1)}, u32[]{:S(2)}, u32[]{:S(2)}) async-start(f32[16,4,4,128]{3,2,1,0:T(4,128)} %bitcast.30), calls=%async_computation.4 | async-start | bytes 262144 | tf_op jit(solution)/shard_map/all_to_all | solution.py:97
  52.8 1.5 broadcast_select_fusion
  54.4 3.6 %all-to-all-done.4 = f32[16,4,4,128]{3,2,1,0:T(4,128)S(1)} async-done(((f32[16,4,4,128]{3,2,1,0:T(4,128)}), f32[16,4,4,128]{3,2,1,0:T(4,128)S(1)}, u32[]{:S(2)}, u32[]{:S(2)}) %all-to-all-start.4) | async-done | bytes 131104 | tf_op jit(solution)/shard_map/all_to_all | solution.py:97
  58.0 7.0 %all-to-all-start.5 = ((bf16[16,4,4,32,128]{4,3,2,1,0:T(8,128)(2,1)}), bf16[16,4,4,32,128]{4,3,2,1,0:T(8,128)(2,1)}, u32[]{:S(2)}, u32[]{:S(2)}) async-start(bf16[16,4,4,32,128]{4,3,2,1,0:T(8,128)(2,1)} %broadcast_select_fusion), calls=%async_computation.5 | async-start | bytes 4194304 | tf_op jit(solution)/shard_map/all_to_all | solution.py:105
  65.6 0.8 gather_fusion
  68.8 43.8 %all-to-all-done.5 = bf16[16,4,4,32,128]{4,3,2,1,0:T(8,128)(2,1)} async-done(((bf16[16,4,4,32,128]{4,3,2,1,0:T(8,128)(2,1)}), bf16[16,4,4,32,128]{4,3,2,1,0:T(8,128)(2,1)}, u32[]{:S(2)}, u32[]{:S(2)}) %all-to-all-start.5) | async-done | bytes 2097184 | tf_op jit(solution)/shard_map/all_to_all | solution.py:105
  112.6 4.8 %all-to-all-start = ((f32[16,1,4]{2,1,0:T(1,128)}), f32[16,1,4]{2,1,0:T(1,128)S(1)}, u32[]{:S(2)}, u32[]{:S(2)}) async-start(f32[16,1,4]{2,1,0:T(1,128)} %copy.61), calls=%async_computation | async-start | bytes 16384 | tf_op jit(solution)/shard_map/all_to_all | solution.py:144
  117.3 3.3 %gather_fusion.2 = bf16[32,4,32,128]{3,2,1,0:T(8,128)(2,1)} fusion(bf16[64,4,32,128]{3,2,1,0:T(8,128)(2,1)} %bitcast.37, s32[1024]{0:T(1024)S(1)} %pad_clamp_fusion.3), kind=kCustom, calls=%fused_computation.8 | custom fusion | bytes 2097280 | tf_op jit(solution)/shard_map/jit(_take)/gather | solution.py:106
  120.6 2.4 broadcast_select_fusion.1
  123.0 18.8 %while.14 = (s32[]{:T(128)}, f32[4,8,4,128]{3,2,1,0:T(4,128)S(1)}, f32[4,8,4,128]{3,2,1,0:T(4,128)S(1)}, f32[4,8,4,32,128]{4,3,2,1,0:T(8,128)S(1)}, s32[4,8,4,12...) while((s32[]{:T(128)}, f32[4,8,4,128]{3,2,1,0:T(4,128)S(1)}, ...), condition=%wide.region_9.12_spmd, body=%wide.region_6.11_spmd.sunk | while | flops 45473792 | bytes 1657973 | solution.py:114
  124.0 0.7 fusion.48
  124.7 1.0 fusion.49
  125.7 1.9 fusion.50
  127.8 0.7 dynamic-slice_bitcast_fusion.8
  128.7 0.7 fusion.48
  129.4 1.0 fusion.49
  130.4 1.9 fusion.50
  132.5 0.7 dynamic-slice_bitcast_fusion.8
  133.4 0.7 fusion.48
  134.1 1.0 fusion.49
  135.1 1.9 fusion.50
  138.1 0.7 fusion.48
  138.8 1.0 fusion.49
  139.8 1.9 fusion.50
  143.1 0.9 select_select_fusion.1
  144.0 6.0 %all-to-all-start.6 = ((f32[16,4,4,128]{3,2,1,0:T(4,128)}), f32[16,4,4,128]{3,2,1,0:T(4,128)S(1)}, u32[]{:S(2)}, u32[]{:S(2)}) async-start(f32[16,4,4,128]{3,2,1,0:T(4,128)} %bitcast.40), calls=%async_computation.6 | async-start | bytes 262144 | tf_op jit(solution)/shard_map/all_to_all | solution.py:142
  150.4 2.8 gather_fusion.4
  153.2 2.0 all-to-all-done.6
  155.2 6.2 %all-to-all-start.8 = ((f32[16,4,4,128]{3,2,1,0:T(4,128)}), f32[16,4,4,128]{3,2,1,0:T(4,128)S(1)}, u32[]{:S(2)}, u32[]{:S(2)}) async-start(f32[16,4,4,128]{3,2,1,0:T(4,128)} %bitcast.46), calls=%async_computation.8 | async-start | bytes 262144 | tf_op jit(solution)/shard_map/all_to_all | solution.py:143
  161.4 4.7 %select_select_fusion = f32[16,4,4,32,128]{4,3,2,1,0:T(8,128)} fusion(f32[16,4,4,32,128]{4,3,2,1,0:T(8,128)} %bitcast.127, pred[16,4]{1,0:T(8,128)(4,1)S(1)} %copy.70, pred[16,4]{1,0:T(8,128)(4,1)S(1)} %broadcast_in_dim.205), kind=kLoop, calls=%fused_computation.44 | loop fusion | flops 2097152 | bytes 8388736 | tf_op jit(solution)/shard_map/jit(_where)/select_n | solution.py:126
  166.6 7.1 %all-to-all-start.7 = ((f32[16,4,4,32,128]{4,3,2,1,0:T(8,128)}), f32[16,4,4,32,128]{4,3,2,1,0:T(8,128)}, u32[]{:S(2)}, u32[]{:S(2)}) async-start(f32[16,4,4,32,128]{4,3,2,1,0:T(8,128)} %select_select_fusion), calls=%async_computation.7 | async-start | bytes 8388608 | tf_op jit(solution)/shard_map/all_to_all | solution.py:141
  173.9 2.8 scatter_fusion
  177.7 2.8 scatter_fusion.2
  180.5 85.7 %all-to-all-done.7 = f32[16,4,4,32,128]{4,3,2,1,0:T(8,128)} async-done(((f32[16,4,4,32,128]{4,3,2,1,0:T(8,128)}), f32[16,4,4,32,128]{4,3,2,1,0:T(8,128)}, u32[]{:S(2)}, u32[]{:S(2)}) %all-to-all-start.7) | async-done | bytes 4194336 | tf_op jit(solution)/shard_map/all_to_all | solution.py:141
  266.2 5.1 %bitcast_multiply_fusion = f32[64,4,32,128]{3,2,1,0:T(8,128)} fusion(f32[16,4,4,32,128]{4,3,2,1,0:T(8,128)} %all-to-all-done.7, f32[64,4,128]{2,1,0:T(4,128)S(1)} %get-tuple-element.74), kind=kLoop, calls=%fused_computation.43 | loop fusion | flops 1048576 | bytes 8519680 | tf_op jit(solution)/shard_map/mul | solution.py:158
  271.3 8.8 %scatter_fusion.1 = f32[16,4,32,128]{3,2,1,0:T(8,128)S(1)} fusion(f32[16,4,32,128]{3,2,1,0:T(8,128)S(1)} %convert_multiply_fusion, s32[64]{0:T(128)S(1)} %fusion.28, f32[64,4,32,128]{3,2,1,0:T(8,128)} %bitcast_multiply_fusion), kind=kCustom, calls=%fused_computation.12 | custom fusion | flops 1048576 | bytes 12583168 | tf_op jit(solution)/shard_map/scatter-add | solution.py:158
  281.2 1.4 fusion.22
  (130 shorter events, 21.0 us)
Async XLA Ops:
  6.5 24.9 %copy-start = (bf16[128,256]{1,0:T(8,128)(2,1)S(1)}, bf16[128,256]{1,0:T(8,128)(2,1)}, u32[]{:S(2)}) copy-start(bf16[128,256]{1,0:T(8,128)(2,1)} %param.17) | copy-start | bytes 196612
  6.5 24.9 %all-gather.2.cloned.1.call-start = ((), (), s32[]{:S(2)}) async-start(), calls=%async_computation.9 | async-start | bytes 1572864 | tf_op jit(solution)/shard_map/all_gather | solution.py:54
  8.7 11.1 %copy-start.4 = (s32[32]{0:T(128)}, s32[32]{0:T(128)S(1)}, u32[]{:S(2)}) copy-start(s32[32]{0:T(128)S(1)} %get-tuple-element.78) | copy-start | bytes 388
  9.4 10.3 %all-to-all-start.1 = ((s32[16,1,4]{2,1,0:T(1,128)}), s32[16,1,4]{2,1,0:T(1,128)S(1)}, u32[]{:S(2)}, u32[]{:S(2)}) async-start(s32[16,1,4]{2,1,0:T(1,128)} %bitcast.21), calls=%async_computation.1 | async-start | bytes 16384 | tf_op jit(solution)/shard_map/all_to_all | solution.py:86
  17.3 8.4 %copy-start.7 = (s32[32]{0:T(128)}, s32[32]{0:T(128)S(1)}, u32[]{:S(2)}) copy-start(s32[32]{0:T(128)S(1)} %get-tuple-element.76) | copy-start | bytes 388
  19.8 9.9 %all-to-all-start.3 = ((s32[16,1,4]{2,1,0:T(1,128)}), s32[16,1,4]{2,1,0:T(1,128)S(1)}, u32[]{:S(2)}, u32[]{:S(2)}) async-start(s32[16,1,4]{2,1,0:T(1,128)} %bitcast.27), calls=%async_computation.3 | async-start | bytes 16384 | tf_op jit(solution)/shard_map/all_to_all | solution.py:85
  35.2 11.4 %all-to-all-start.2 = ((f32[16,4,4,128]{3,2,1,0:T(4,128)}), f32[16,4,4,128]{3,2,1,0:T(4,128)S(1)}, u32[]{:S(2)}, u32[]{:S(2)}) async-start(f32[16,4,4,128]{3,2,1,0:T(4,128)} %bitcast.24), calls=%async_computation.2 | async-start | bytes 262144 | tf_op jit(solution)/shard_map/all_to_all | solution.py:98
  46.6 11.4 %all-to-all-start.4 = ((f32[16,4,4,128]{3,2,1,0:T(4,128)}), f32[16,4,4,128]{3,2,1,0:T(4,128)S(1)}, u32[]{:S(2)}, u32[]{:S(2)}) async-start(f32[16,4,4,128]{3,2,1,0:T(4,128)} %bitcast.30), calls=%async_computation.4 | async-start | bytes 262144 | tf_op jit(solution)/shard_map/all_to_all | solution.py:97
  54.3 10.7 %copy-start.3 = (pred[32]{0:T(512)(128)(4,1)S(1)}, pred[32]{0:T(512)(128)(4,1)}, u32[]{:S(2)}) copy-start(pred[32]{0:T(512)(128)(4,1)} %get-tuple-element.75) | copy-start | bytes 100
  54.3 10.8 %copy-start.5 = (s32[32]{0:T(128)S(1)}, s32[32]{0:T(128)}, u32[]{:S(2)}) copy-start(s32[32]{0:T(128)} %copy-done.4) | copy-start | bytes 388
  54.3 12.9 %copy-start.8 = (s32[32]{0:T(128)S(1)}, s32[32]{0:T(128)}, u32[]{:S(2)}) copy-start(s32[32]{0:T(128)} %copy-done.7) | copy-start | bytes 388
  54.4 14.3 %copy-start.2 = (pred[32]{0:T(512)(128)(4,1)S(1)}, pred[32]{0:T(512)(128)(4,1)}, u32[]{:S(2)}) copy-start(pred[32]{0:T(512)(128)(4,1)} %get-tuple-element.77) | copy-start | bytes 100
  58.0 54.6 %all-to-all-start.5 = ((bf16[16,4,4,32,128]{4,3,2,1,0:T(8,128)(2,1)}), bf16[16,4,4,32,128]{4,3,2,1,0:T(8,128)(2,1)}, u32[]{:S(2)}, u32[]{:S(2)}) async-start(bf16[16,4,4,32,128]{4,3,2,1,0:T(8,128)(2,1)} %broadcast_select_fusion), calls=%async_computation.5 | async-start | bytes 4194304 | tf_op jit(solution)/shard_map/all_to_all | solution.py:105
  112.6 31.4 %all-to-all-start = ((f32[16,1,4]{2,1,0:T(1,128)}), f32[16,1,4]{2,1,0:T(1,128)S(1)}, u32[]{:S(2)}, u32[]{:S(2)}) async-start(f32[16,1,4]{2,1,0:T(1,128)} %copy.61), calls=%async_computation | async-start | bytes 16384 | tf_op jit(solution)/shard_map/all_to_all | solution.py:144
  144.0 11.2 %all-to-all-start.6 = ((f32[16,4,4,128]{3,2,1,0:T(4,128)}), f32[16,4,4,128]{3,2,1,0:T(4,128)S(1)}, u32[]{:S(2)}, u32[]{:S(2)}) async-start(f32[16,4,4,128]{3,2,1,0:T(4,128)} %bitcast.40), calls=%async_computation.6 | async-start | bytes 262144 | tf_op jit(solution)/shard_map/all_to_all | solution.py:142
  155.2 11.4 %all-to-all-start.8 = ((f32[16,4,4,128]{3,2,1,0:T(4,128)}), f32[16,4,4,128]{3,2,1,0:T(4,128)S(1)}, u32[]{:S(2)}, u32[]{:S(2)}) async-start(f32[16,4,4,128]{3,2,1,0:T(4,128)} %bitcast.46), calls=%async_computation.8 | async-start | bytes 262144 | tf_op jit(solution)/shard_map/all_to_all | solution.py:143
  166.6 99.6 %all-to-all-start.7 = ((f32[16,4,4,32,128]{4,3,2,1,0:T(8,128)}), f32[16,4,4,32,128]{4,3,2,1,0:T(8,128)}, u32[]{:S(2)}, u32[]{:S(2)}) async-start(f32[16,4,4,32,128]{4,3,2,1,0:T(8,128)} %select_select_fusion), calls=%async_computation.7 | async-start | bytes 8388608 | tf_op jit(solution)/shard_map/all_to_all | solution.py:141
  280.1 1.0 copy-start.1
  280.1 1.0 copy-start.6
Sparse Core Ops, SparseCore 0:
  8.9 22.2 all-gather.1
where the time goes:
time: 291 us; the launch traced here: 289 us
  waiting for transfers between devices  140 us (48%)
  starting transfers between devices  56.1 us (19%)
  other arithmetic  46.2 us (16%)
  local copies, waits for them, and re-layouts  22.2 us (8%)
  between operations  13.8 us (5%)
  matrix products  10.6 us (4%)
    all_to_all x1, waiting for transfers between devices, local(): lax.all_to_all(send_values, 'dp', split_axis=0, concat_axis=0, tiled=True)  85.7 us
    all_to_all x1, waiting for transfers between devices, local(): lax.all_to_all(send_feats, 'dp', split_axis=0, concat_axis=0, tiled=True)  43.8 us
    scatter-add x1, other arithmetic, local(): summed = (self_weight[:, :, None, :] * feat_blocks.astype(jnp.float32)).a...  8.79 us
    dot_general x4, matrix products, tile_group(): jnp.einsum('ghdc,ghcr->ghdr', feats_here, weights.astype(jnp.bfloat16), p...  7.77 us
    all_to_all x1, starting transfers between devices, local(): lax.all_to_all(send_values, 'dp', split_axis=0, concat_axis=0, tiled=True)  7.15 us
    all_to_all x1, starting transfers between devices, local(): lax.all_to_all(send_feats, 'dp', split_axis=0, concat_axis=0, tiled=True)  7.04 us
    all_to_all x1, starting transfers between devices, local(): lax.all_to_all(to_slots(row_slot, row_local), 'dp', split_axis=0, concat_...  6.52 us
    all_to_all x1, starting transfers between devices, local(): lax.all_to_all(send_target, 'dp', split_axis=0, concat_axis=0, tiled=True)  6.25 us
  transfers between devices with their start and end apart: 10, of which 8 were waited for; matrix products, arithmetic and copies ran while one was open for 20% of the time, Pallas kernels for 0%

commit v1 on v0

--- a/solution.py
+++ b/solution.py
@@ -102,7 +102,19 @@
     send_feats = jnp.take(feat_blocks, wanted.reshape(-1), axis=0).reshape(
         devices_dp, capacity, local_heads, HD, tile_size
     )
-    got_feats = lax.all_to_all(send_feats, "dp", split_axis=0, concat_axis=0, tiled=True)
+    ways, here = (lax.axis_size("dp"), lax.axis_index("dp"))
+    width = send_feats.shape[0] // ways
+    dims = list(send_feats.shape)
+    dims[0] = width
+    height = dims[0]
+    dims[0] = height * ways
+    full = jnp.zeros(dims, send_feats.dtype)
+    for mask in range(ways):
+        part = lax.dynamic_slice_in_dim(send_feats, (here ^ mask) * width, width, axis=0)
+        if mask:
+            part = lax.ppermute(part, "dp", [(d, d ^ mask) for d in range(ways)])
+        full = lax.dynamic_update_slice_in_dim(full, part, (here ^ mask) * height, axis=0)
+    got_feats = full
     tile_feats = jnp.take(
         got_feats.reshape(slot_count, local_heads, HD, tile_size), col_slot, axis=0
     )

time: 291 us -> 305 us (1.048)
  waiting for transfers between devices: 140 us -> 110 us
  starting transfers between devices: 56.1 us -> 82.6 us
  local copies, waits for them, and re-layouts: 22.2 us -> 41.7 us
    all_to_all x1 -> x0, waiting for transfers between devices: 43.8 us -> none  [local(): lax.all_to_all(send_feats, 'dp', split_axis=0, concat_axis=0, tiled=True)]
    ppermute x0 -> x15, starting transfers between devices: none -> 30.1 us  [local(): part = lax.ppermute(part, 'dp', [(d, d ^ mask) for d in range(ways)])]
    ppermute x0 -> x15, waiting for transfers between devices: none -> 14.9 us  [local(): part = lax.ppermute(part, 'dp', [(d, d ^ mask) for d in range(ways)])]
    dynamic_update_slice x0 -> x15, local copies, waits for them, and re-layouts: none -> 14.4 us  [local(): lax.dynamic_update_slice_in_dim(full, part, (here ^ mask) * height, axis=0)]
    all_to_all x1 -> x0, starting transfers between devices: 7.04 us -> none  [local(): lax.all_to_all(send_feats, 'dp', split_axis=0, concat_axis=0, tiled=True)]
    all_to_all x1, waiting for transfers between devices: 3.65 us -> 0.01 us  [local(): lax.all_to_all(send_source, 'dp', split_axis=0, concat_axis=0, tiled=True)]
    all_to_all x1, waiting for transfers between devices: 0.16 us -> 3.77 us  [local(): lax.all_to_all(to_slots(row_slot, row_local), 'dp', split_axis=0, concat_...]
  transfers between devices with their start and end apart: 10 -> 24, of which waited for: 8 -> 13; matrix products, arithmetic and copies ran while one was open for 20% -> 24% of each run, Pallas kernels for 0% -> 0%
where the time goes in v1:
time: 305 us; the launch traced here: 304 us
  waiting for transfers between devices  110 us (36%)
  starting transfers between devices  82.6 us (27%)
  other arithmetic  44.6 us (15%)
  local copies, waits for them, and re-layouts  41.7 us (14%)
  between operations  13.8 us (5%)
  matrix products  10.6 us (3%)
    all_to_all x1, waiting for transfers between devices, local(): lax.all_to_all(send_values, 'dp', split_axis=0, concat_axis=0, tiled=True)  85.7 us
    ppermute x15, starting transfers between devices, local(): part = lax.ppermute(part, 'dp', [(d, d ^ mask) for d in range(ways)])  30.1 us
    ppermute x15, waiting for transfers between devices, local(): part = lax.ppermute(part, 'dp', [(d, d ^ mask) for d in range(ways)])  14.9 us
    dynamic_update_slice x15, local copies, waits for them, and re-layouts, local(): lax.dynamic_update_slice_in_dim(full, part, (here ^ mask) * height, axis=0)  14.4 us
    scatter-add x1, other arithmetic, local(): summed = (self_weight[:, :, None, :] * feat_blocks.astype(jnp.float32)).a...  8.79 us
    all_to_all x1, starting transfers between devices, local(): lax.all_to_all(send_target, 'dp', split_axis=0, concat_axis=0, tiled=True)  8.43 us
    dot_general x4, matrix products, tile_group(): jnp.einsum('ghdc,ghcr->ghdr', feats_here, weights.astype(jnp.bfloat16), p...  7.77 us
    all_to_all x1, starting transfers between devices, local(): lax.all_to_all(send_values, 'dp', split_axis=0, concat_axis=0, tiled=True)  7.15 us
  transfers between devices with their start and end apart: 24, of which 13 were waited for; matrix products, arithmetic and copies ran while one was open for 24% of the time, Pallas kernels for 0%

profile of v1, /device:TPU:11, one launch (start us, length us, event | category | flops | bytes accessed | tf_op | source)
XLA Modules:
  0.0 303.6 jit_solution(13165555043327714131)
XLA Ops:
  8.9 6.5 %all-to-all-start.3 = ((s32[16,1,4]{2,1,0:T(1,128)}), s32[16,1,4]{2,1,0:T(1,128)S(1)}, u32[]{:S(2)}, u32[]{:S(2)}) async-start(s32[16,1,4]{2,1,0:T(1,128)} %bitcast.27), calls=%async_computation.3 | async-start | bytes 16384 | tf_op jit(solution)/shard_map/all_to_all | solution.py:85
  22.1 6.0 %all-to-all-start.1 = ((s32[16,1,4]{2,1,0:T(1,128)}), s32[16,1,4]{2,1,0:T(1,128)S(1)}, u32[]{:S(2)}, u32[]{:S(2)}) async-start(s32[16,1,4]{2,1,0:T(1,128)} %bitcast.21), calls=%async_computation.1 | async-start | bytes 16384 | tf_op jit(solution)/shard_map/all_to_all | solution.py:86
  28.2 3.8 %all-to-all-done.1 = s32[16,1,4]{2,1,0:T(1,128)S(1)} async-done(((s32[16,1,4]{2,1,0:T(1,128)}), s32[16,1,4]{2,1,0:T(1,128)S(1)}, u32[]{:S(2)}, u32[]{:S(2)}) %all-to-all-start.1) | async-done | bytes 288 | tf_op jit(solution)/shard_map/all_to_all | solution.py:86
  34.3 1.5 fusion.30
  38.8 6.0 %all-to-all-start.4 = ((f32[16,4,4,128]{3,2,1,0:T(4,128)}), f32[16,4,4,128]{3,2,1,0:T(4,128)S(1)}, u32[]{:S(2)}, u32[]{:S(2)}) async-start(f32[16,4,4,128]{3,2,1,0:T(4,128)} %bitcast.30), calls=%async_computation.4 | async-start | bytes 262144 | tf_op jit(solution)/shard_map/all_to_all | solution.py:97
  45.1 2.1 gather_fusion.1
  47.2 1.8 broadcast_select_fusion
  49.6 1.4 constant_dynamic-slice_fusion
  51.0 1.3 copy-done.1
  52.4 1.5 collective-permute-start.14
  55.0 1.5 collective-permute-start.12
  59.9 1.6 constant_dynamic-update-slice_fusion.14
  61.9 5.0 %collective-permute-start.3 = (bf16[1,4,4,32,128]{4,3,2,1,0:T(8,128)(2,1)}, bf16[1,4,4,32,128]{4,3,2,1,0:T(8,128)(2,1)S(1)}, u32[]{:S(2)}, u32[]{:S(2)}) collective-permute-start(bf16[1,4,4,32,128]{4,3,2,1,0:T(8,128)(2,1)} %get-tuple-element.92), channel_id=1, source_target_pairs={{0,8},{2,10},{4,12},{6,14},{8,0},{10,2},{12,4},{14,6},{16,24},{18,... | collective-permute-start | bytes 393224 | tf_op jit(solution)/shard_map/ppermute | solution.py:115
  66.9 1.6 constant_dynamic-update-slice_fusion.13
  68.5 1.4 collective-permute-start.4
  70.6 2.2 collective-permute-start.5
  74.5 2.2 collective-permute-start.6
  79.7 2.0 collective-permute-done.6
  81.7 2.1 collective-permute-start.8
  84.8 8.2 %collective-permute-start.9 = (bf16[1,4,4,32,128]{4,3,2,1,0:T(8,128)(2,1)S(1)}, bf16[1,4,4,32,128]{4,3,2,1,0:T(8,128)(2,1)S(1)}, u32[]{:S(2)}, u32[]{:S(2)}) collective-permute-start(bf16[1,4,4,32,128]{4,3,2,1,0:T(8,128)(2,1)S(1)} %copy-done.6), channel_id=1, source_target_pairs={{0,20},{2,22},{4,16},{6,18},{8,28},{10,30},{12,24},{14,26},{16,4},... | collective-permute-start | bytes 393224 | tf_op jit(solution)/shard_map/ppermute | solution.py:115
  93.6 2.5 collective-permute-start.10
  98.5 3.7 %collective-permute-done.10 = bf16[1,4,4,32,128]{4,3,2,1,0:T(8,128)(2,1)S(1)} collective-permute-done((bf16[1,4,4,32,128]{4,3,2,1,0:T(8,128)(2,1)S(1)}, bf16[1,4,4,32,128]{4,3,2,1,0:T(8,128)(2,1)S(1)}, u32[]{:S(2)}, u32[]{:S(2)}) %collective-permute-start.10) | collective-permute-done | bytes 131104 | tf_op jit(solution)/shard_map/ppermute | solution.py:115
  102.8 5.1 %collective-permute-done.11 = bf16[1,4,4,32,128]{4,3,2,1,0:T(8,128)(2,1)S(1)} collective-permute-done((bf16[1,4,4,32,128]{4,3,2,1,0:T(8,128)(2,1)S(1)}, bf16[1,4,4,32,128]{4,3,2,1,0:T(8,128)(2,1)S(1)}, u32[]{:S(2)}, u32[]{:S(2)}) %collective-permute-start.11) | collective-permute-done | bytes 131104 | tf_op jit(solution)/shard_map/ppermute | solution.py:115
  108.6 1.6 constant_dynamic-update-slice_fusion.2
  110.1 1.6 constant_dynamic-update-slice_fusion.1
  111.7 1.6 constant_dynamic-update-slice_fusion
  113.3 3.3 %gather_fusion.2 = bf16[32,4,32,128]{3,2,1,0:T(8,128)(2,1)} fusion(bf16[64,4,32,128]{3,2,1,0:T(8,128)(2,1)} %bitcast.131, s32[1024]{0:T(1024)S(1)} %pad_clamp_fusion.3), kind=kCustom, calls=%fused_computation.8 | custom fusion | bytes 2097280 | tf_op jit(solution)/shard_map/jit(_take)/gather | solution.py:118
  116.5 8.4 %all-to-all-start.2 = ((f32[16,4,4,128]{3,2,1,0:T(4,128)}), f32[16,4,4,128]{3,2,1,0:T(4,128)S(1)}, u32[]{:S(2)}, u32[]{:S(2)}) async-start(f32[16,4,4,128]{3,2,1,0:T(4,128)} %bitcast.24), calls=%async_computation.2 | async-start | bytes 262144 | tf_op jit(solution)/shard_map/all_to_all | solution.py:98
  125.0 2.4 broadcast_select_fusion.1
  128.0 2.1 all-to-all-done.2
  130.1 6.1 %all-to-all-start = ((f32[16,1,4]{2,1,0:T(1,128)}), f32[16,1,4]{2,1,0:T(1,128)S(1)}, u32[]{:S(2)}, u32[]{:S(2)}) async-start(f32[16,1,4]{2,1,0:T(1,128)} %copy.61), calls=%async_computation | async-start | bytes 16384 | tf_op jit(solution)/shard_map/all_to_all | solution.py:156
  137.0 18.8 %while.14 = (s32[]{:T(128)}, f32[4,8,4,128]{3,2,1,0:T(4,128)S(1)}, f32[4,8,4,128]{3,2,1,0:T(4,128)S(1)}, f32[4,8,4,32,128]{4,3,2,1,0:T(8,128)S(1)}, s32[4,8,4,12...) while((s32[]{:T(128)}, f32[4,8,4,128]{3,2,1,0:T(4,128)S(1)}, ...), condition=%wide.region_9.12_spmd, body=%wide.region_6.11_spmd.sunk | while | flops 45473792 | bytes 1657973 | solution.py:126
  139.8 1.9 fusion.50
  144.5 1.9 fusion.50
  149.2 1.9 fusion.50
  153.9 1.9 fusion.50
  158.1 6.1 %all-to-all-start.5 = ((f32[16,4,4,128]{3,2,1,0:T(4,128)}), f32[16,4,4,128]{3,2,1,0:T(4,128)S(1)}, u32[]{:S(2)}, u32[]{:S(2)}) async-start(f32[16,4,4,128]{3,2,1,0:T(4,128)} %bitcast.40), calls=%async_computation.5 | async-start | bytes 262144 | tf_op jit(solution)/shard_map/all_to_all | solution.py:154
  164.3 2.8 gather_fusion.4
  167.1 2.2 all-to-all-done.5
  169.3 6.2 %all-to-all-start.7 = ((f32[16,4,4,128]{3,2,1,0:T(4,128)}), f32[16,4,4,128]{3,2,1,0:T(4,128)S(1)}, u32[]{:S(2)}, u32[]{:S(2)}) async-start(f32[16,4,4,128]{3,2,1,0:T(4,128)} %bitcast.46), calls=%async_computation.7 | async-start | bytes 262144 | tf_op jit(solution)/shard_map/all_to_all | solution.py:155
  175.5 4.6 %select_select_fusion = f32[16,4,4,32,128]{4,3,2,1,0:T(8,128)} fusion(f32[16,4,4,32,128]{4,3,2,1,0:T(8,128)} %bitcast.127, pred[16,4]{1,0:T(8,128)(4,1)S(1)} %copy.70, pred[16,4]{1,0:T(8,128)(4,1)S(1)} %broadcast_in_dim.209), kind=kLoop, calls=%fused_computation.44 | loop fusion | flops 2097152 | bytes 8388736 | tf_op jit(solution)/shard_map/jit(_where)/select_n | solution.py:138
  180.7 7.2 %all-to-all-start.6 = ((f32[16,4,4,32,128]{4,3,2,1,0:T(8,128)}), f32[16,4,4,32,128]{4,3,2,1,0:T(8,128)}, u32[]{:S(2)}, u32[]{:S(2)}) async-start(f32[16,4,4,32,128]{4,3,2,1,0:T(8,128)} %select_select_fusion), calls=%async_computation.6 | async-start | bytes 8388608 | tf_op jit(solution)/shard_map/all_to_all | solution.py:153
  188.0 2.8 scatter_fusion
  191.8 2.8 scatter_fusion.2
  194.6 85.7 %all-to-all-done.6 = f32[16,4,4,32,128]{4,3,2,1,0:T(8,128)} async-done(((f32[16,4,4,32,128]{4,3,2,1,0:T(8,128)}), f32[16,4,4,32,128]{4,3,2,1,0:T(8,128)}, u32[]{:S(2)}, u32[]{:S(2)}) %all-to-all-start.6) | async-done | bytes 4194336 | tf_op jit(solution)/shard_map/all_to_all | solution.py:153
  280.3 5.1 %bitcast_multiply_fusion = f32[64,4,32,128]{3,2,1,0:T(8,128)} fusion(f32[16,4,4,32,128]{4,3,2,1,0:T(8,128)} %all-to-all-done.6, f32[64,4,128]{2,1,0:T(4,128)S(1)} %get-tuple-element.74), kind=kLoop, calls=%fused_computation.43 | loop fusion | flops 1048576 | bytes 8519680 | tf_op jit(solution)/shard_map/mul | solution.py:170
  285.4 8.8 %scatter_fusion.1 = f32[16,4,32,128]{3,2,1,0:T(8,128)S(1)} fusion(f32[16,4,32,128]{3,2,1,0:T(8,128)S(1)} %convert_multiply_fusion, s32[64]{0:T(128)S(1)} %fusion.28, f32[64,4,32,128]{3,2,1,0:T(8,128)} %bitcast_multiply_fusion), kind=kCustom, calls=%fused_computation.12 | custom fusion | flops 1048576 | bytes 12583168 | tf_op jit(solution)/shard_map/scatter-add | solution.py:170
  295.3 1.4 fusion.22
  (174 shorter events, 48.0 us)
Async XLA Ops:
  6.5 27.8 %copy-start = (bf16[128,256]{1,0:T(8,128)(2,1)S(1)}, bf16[128,256]{1,0:T(8,128)(2,1)}, u32[]{:S(2)}) copy-start(bf16[128,256]{1,0:T(8,128)(2,1)} %param.17) | copy-start | bytes 196612
  6.5 27.8 %all-gather.2.cloned.1.call-start = ((), (), s32[]{:S(2)}) async-start(), calls=%async_computation.8 | async-start | bytes 1572864 | tf_op jit(solution)/shard_map/all_gather | solution.py:54
  8.9 13.2 %all-to-all-start.3 = ((s32[16,1,4]{2,1,0:T(1,128)}), s32[16,1,4]{2,1,0:T(1,128)S(1)}, u32[]{:S(2)}, u32[]{:S(2)}) async-start(s32[16,1,4]{2,1,0:T(1,128)} %bitcast.27), calls=%async_computation.3 | async-start | bytes 16384 | tf_op jit(solution)/shard_map/all_to_all | solution.py:85
  22.1 9.9 %all-to-all-start.1 = ((s32[16,1,4]{2,1,0:T(1,128)}), s32[16,1,4]{2,1,0:T(1,128)S(1)}, u32[]{:S(2)}, u32[]{:S(2)}) async-start(s32[16,1,4]{2,1,0:T(1,128)} %bitcast.21), calls=%async_computation.1 | async-start | bytes 16384 | tf_op jit(solution)/shard_map/all_to_all | solution.py:86
  38.8 77.7 %all-to-all-start.4 = ((f32[16,4,4,128]{3,2,1,0:T(4,128)}), f32[16,4,4,128]{3,2,1,0:T(4,128)S(1)}, u32[]{:S(2)}, u32[]{:S(2)}) async-start(f32[16,4,4,128]{3,2,1,0:T(4,128)} %bitcast.30), calls=%async_computation.4 | async-start | bytes 262144 | tf_op jit(solution)/shard_map/all_to_all | solution.py:97
  51.0 1.3 copy-start.1
  52.4 59.3 %collective-permute-start.14 = (bf16[1,4,4,32,128]{4,3,2,1,0:T(8,128)(2,1)S(1)}, bf16[1,4,4,32,128]{4,3,2,1,0:T(8,128)(2,1)}, u32[]{:S(2)}, u32[]{:S(2)}) collective-permute-start(bf16[1,4,4,32,128]{4,3,2,1,0:T(8,128)(2,1)S(1)} %get-tuple-element.81), channel_id=1, source_target_pairs={{0,30},{2,28},{4,26},{6,24},{8,22},{10,20},{12,18},{14,16},{16,14}... | collective-permute-start | bytes 393224 | tf_op jit(solution)/shard_map/ppermute | solution.py:115
  53.8 56.3 %collective-permute-start.13 = (bf16[1,4,4,32,128]{4,3,2,1,0:T(8,128)(2,1)S(1)}, bf16[1,4,4,32,128]{4,3,2,1,0:T(8,128)(2,1)}, u32[]{:S(2)}, u32[]{:S(2)}) collective-permute-start(bf16[1,4,4,32,128]{4,3,2,1,0:T(8,128)(2,1)S(1)} %get-tuple-element.82), channel_id=1, source_target_pairs={{0,28},{2,30},{4,24},{6,26},{8,20},{10,22},{12,16},{14,18},{16,12}... | collective-permute-start | bytes 393224 | tf_op jit(solution)/shard_map/ppermute | solution.py:115
  55.0 53.6 %collective-permute-start.12 = (bf16[1,4,4,32,128]{4,3,2,1,0:T(8,128)(2,1)S(1)}, bf16[1,4,4,32,128]{4,3,2,1,0:T(8,128)(2,1)}, u32[]{:S(2)}, u32[]{:S(2)}) collective-permute-start(bf16[1,4,4,32,128]{4,3,2,1,0:T(8,128)(2,1)S(1)} %get-tuple-element.83), channel_id=1, source_target_pairs={{0,26},{2,24},{4,30},{6,28},{8,18},{10,16},{12,22},{14,20},{16,10}... | collective-permute-start | bytes 393224 | tf_op jit(solution)/shard_map/ppermute | solution.py:115
  56.5 5.4 %collective-permute-start.1 = (bf16[1,4,4,32,128]{4,3,2,1,0:T(8,128)(2,1)}, bf16[1,4,4,32,128]{4,3,2,1,0:T(8,128)(2,1)}, u32[]{:S(2)}, u32[]{:S(2)}) collective-permute-start(bf16[1,4,4,32,128]{4,3,2,1,0:T(8,128)(2,1)} %get-tuple-element.94), channel_id=1, source_target_pairs={{0,4},{2,6},{4,0},{6,2},{8,12},{10,14},{12,8},{14,10},{16,20},{18,... | collective-permute-start | bytes 393224 | tf_op jit(solution)/shard_map/ppermute | solution.py:115
  56.8 1.9 collective-permute-start
  57.8 27.0 %copy-start.6 = (bf16[1,4,4,32,128]{4,3,2,1,0:T(8,128)(2,1)S(1)}, bf16[1,4,4,32,128]{4,3,2,1,0:T(8,128)(2,1)}, u32[]{:S(2)}) copy-start(bf16[1,4,4,32,128]{4,3,2,1,0:T(8,128)(2,1)} %get-tuple-element.86) | copy-start | bytes 393220
  57.8 35.8 %copy-start.5 = (bf16[1,4,4,32,128]{4,3,2,1,0:T(8,128)(2,1)S(1)}, bf16[1,4,4,32,128]{4,3,2,1,0:T(8,128)(2,1)}, u32[]{:S(2)}) copy-start(bf16[1,4,4,32,128]{4,3,2,1,0:T(8,128)(2,1)} %get-tuple-element.85) | copy-start | bytes 393220
  57.8 40.0 %copy-start.4 = (bf16[1,4,4,32,128]{4,3,2,1,0:T(8,128)(2,1)S(1)}, bf16[1,4,4,32,128]{4,3,2,1,0:T(8,128)(2,1)}, u32[]{:S(2)}) copy-start(bf16[1,4,4,32,128]{4,3,2,1,0:T(8,128)(2,1)} %get-tuple-element.84) | copy-start | bytes 393220
  58.6 9.9 %collective-permute-start.2 = (bf16[1,4,4,32,128]{4,3,2,1,0:T(8,128)(2,1)}, bf16[1,4,4,32,128]{4,3,2,1,0:T(8,128)(2,1)S(1)}, u32[]{:S(2)}, u32[]{:S(2)}) collective-permute-start(bf16[1,4,4,32,128]{4,3,2,1,0:T(8,128)(2,1)} %get-tuple-element.93), channel_id=1, source_target_pairs={{0,6},{2,4},{4,2},{6,0},{8,14},{10,12},{12,10},{14,8},{16,22},{18,... | collective-permute-start | bytes 393224 | tf_op jit(solution)/shard_map/ppermute | solution.py:115
  61.9 8.7 %collective-permute-start.3 = (bf16[1,4,4,32,128]{4,3,2,1,0:T(8,128)(2,1)}, bf16[1,4,4,32,128]{4,3,2,1,0:T(8,128)(2,1)S(1)}, u32[]{:S(2)}, u32[]{:S(2)}) collective-permute-start(bf16[1,4,4,32,128]{4,3,2,1,0:T(8,128)(2,1)} %get-tuple-element.92), channel_id=1, source_target_pairs={{0,8},{2,10},{4,12},{6,14},{8,0},{10,2},{12,4},{14,6},{16,24},{18,... | collective-permute-start | bytes 393224 | tf_op jit(solution)/shard_map/ppermute | solution.py:115
  68.5 6.0 %collective-permute-start.4 = (bf16[1,4,4,32,128]{4,3,2,1,0:T(8,128)(2,1)}, bf16[1,4,4,32,128]{4,3,2,1,0:T(8,128)(2,1)S(1)}, u32[]{:S(2)}, u32[]{:S(2)}) collective-permute-start(bf16[1,4,4,32,128]{4,3,2,1,0:T(8,128)(2,1)} %get-tuple-element.91), channel_id=1, source_target_pairs={{0,10},{2,8},{4,14},{6,12},{8,2},{10,0},{12,6},{14,4},{16,26},{18,... | collective-permute-start | bytes 393224 | tf_op jit(solution)/shard_map/ppermute | solution.py:115
  70.6 8.1 %collective-permute-start.5 = (bf16[1,4,4,32,128]{4,3,2,1,0:T(8,128)(2,1)}, bf16[1,4,4,32,128]{4,3,2,1,0:T(8,128)(2,1)S(1)}, u32[]{:S(2)}, u32[]{:S(2)}) collective-permute-start(bf16[1,4,4,32,128]{4,3,2,1,0:T(8,128)(2,1)} %get-tuple-element.90), channel_id=1, source_target_pairs={{0,12},{2,14},{4,8},{6,10},{8,4},{10,6},{12,0},{14,2},{16,28},{18,... | collective-permute-start | bytes 393224 | tf_op jit(solution)/shard_map/ppermute | solution.py:115
  74.5 7.2 %collective-permute-start.6 = (bf16[1,4,4,32,128]{4,3,2,1,0:T(8,128)(2,1)}, bf16[1,4,4,32,128]{4,3,2,1,0:T(8,128)(2,1)S(1)}, u32[]{:S(2)}, u32[]{:S(2)}) collective-permute-start(bf16[1,4,4,32,128]{4,3,2,1,0:T(8,128)(2,1)} %get-tuple-element.89), channel_id=1, source_target_pairs={{0,14},{2,12},{4,10},{6,8},{8,6},{10,4},{12,2},{14,0},{16,30},{18,... | collective-permute-start | bytes 393224 | tf_op jit(solution)/shard_map/ppermute | solution.py:115
  78.7 6.1 %collective-permute-start.7 = (bf16[1,4,4,32,128]{4,3,2,1,0:T(8,128)(2,1)}, bf16[1,4,4,32,128]{4,3,2,1,0:T(8,128)(2,1)S(1)}, u32[]{:S(2)}, u32[]{:S(2)}) collective-permute-start(bf16[1,4,4,32,128]{4,3,2,1,0:T(8,128)(2,1)} %get-tuple-element.88), channel_id=1, source_target_pairs={{0,16},{2,18},{4,20},{6,22},{8,24},{10,26},{12,28},{14,30},{16,0},... | collective-permute-start | bytes 393224 | tf_op jit(solution)/shard_map/ppermute | solution.py:115
  81.7 12.0 %collective-permute-start.8 = (bf16[1,4,4,32,128]{4,3,2,1,0:T(8,128)(2,1)}, bf16[1,4,4,32,128]{4,3,2,1,0:T(8,128)(2,1)S(1)}, u32[]{:S(2)}, u32[]{:S(2)}) collective-permute-start(bf16[1,4,4,32,128]{4,3,2,1,0:T(8,128)(2,1)} %get-tuple-element.87), channel_id=1, source_target_pairs={{0,18},{2,16},{4,22},{6,20},{8,26},{10,24},{12,30},{14,28},{16,2},... | collective-permute-start | bytes 393224 | tf_op jit(solution)/shard_map/ppermute | solution.py:115
  84.8 13.1 %collective-permute-start.9 = (bf16[1,4,4,32,128]{4,3,2,1,0:T(8,128)(2,1)S(1)}, bf16[1,4,4,32,128]{4,3,2,1,0:T(8,128)(2,1)S(1)}, u32[]{:S(2)}, u32[]{:S(2)}) collective-permute-start(bf16[1,4,4,32,128]{4,3,2,1,0:T(8,128)(2,1)S(1)} %copy-done.6), channel_id=1, source_target_pairs={{0,20},{2,22},{4,16},{6,18},{8,28},{10,30},{12,24},{14,26},{16,4},... | collective-permute-start | bytes 393224 | tf_op jit(solution)/shard_map/ppermute | solution.py:115
  93.6 31.3 %copy-start.8 = (pred[4,8]{1,0:T(4,128)(4,1)S(1)}, pred[4,8]{1,0:T(4,128)(4,1)}, u32[]{:S(2)}) copy-start(pred[4,8]{1,0:T(4,128)(4,1)} %broadcast_in_dim.201) | copy-start | bytes 100
  93.6 8.5 %collective-permute-start.10 = (bf16[1,4,4,32,128]{4,3,2,1,0:T(8,128)(2,1)S(1)}, bf16[1,4,4,32,128]{4,3,2,1,0:T(8,128)(2,1)S(1)}, u32[]{:S(2)}, u32[]{:S(2)}) collective-permute-start(bf16[1,4,4,32,128]{4,3,2,1,0:T(8,128)(2,1)S(1)} %copy-done.5), channel_id=1, source_target_pairs={{0,22},{2,20},{4,18},{6,16},{8,30},{10,28},{12,26},{14,24},{16,6},... | collective-permute-start | bytes 393224 | tf_op jit(solution)/shard_map/ppermute | solution.py:115
  97.8 10.1 %collective-permute-start.11 = (bf16[1,4,4,32,128]{4,3,2,1,0:T(8,128)(2,1)S(1)}, bf16[1,4,4,32,128]{4,3,2,1,0:T(8,128)(2,1)S(1)}, u32[]{:S(2)}, u32[]{:S(2)}) collective-permute-start(bf16[1,4,4,32,128]{4,3,2,1,0:T(8,128)(2,1)S(1)} %copy-done.4), channel_id=1, source_target_pairs={{0,24},{2,26},{4,28},{6,30},{8,16},{10,18},{12,20},{14,22},{16,8},... | collective-permute-start | bytes 393224 | tf_op jit(solution)/shard_map/ppermute | solution.py:115
  113.2 23.7 %copy-start.3 = (f32[4,8,4,128]{3,2,1,0:T(4,128)S(1)}, f32[4,8,4,128]{3,2,1,0:T(4,128)}, u32[]{:S(2)}) copy-start(f32[4,8,4,128]{3,2,1,0:T(4,128)} %custom-call.22) | copy-start | bytes 196612
  116.5 13.6 %all-to-all-start.2 = ((f32[16,4,4,128]{3,2,1,0:T(4,128)}), f32[16,4,4,128]{3,2,1,0:T(4,128)S(1)}, u32[]{:S(2)}, u32[]{:S(2)}) async-start(f32[16,4,4,128]{3,2,1,0:T(4,128)} %bitcast.24), calls=%async_computation.2 | async-start | bytes 262144 | tf_op jit(solution)/shard_map/all_to_all | solution.py:98
  130.1 27.9 %all-to-all-start = ((f32[16,1,4]{2,1,0:T(1,128)}), f32[16,1,4]{2,1,0:T(1,128)S(1)}, u32[]{:S(2)}, u32[]{:S(2)}) async-start(f32[16,1,4]{2,1,0:T(1,128)} %copy.61), calls=%async_computation | async-start | bytes 16384 | tf_op jit(solution)/shard_map/all_to_all | solution.py:156
  137.0 20.2 %copy-start.9 = (pred[64]{0:T(512)(128)(4,1)S(1)}, pred[64]{0:T(512)(128)(4,1)}, u32[]{:S(2)}) copy-start(pred[64]{0:T(512)(128)(4,1)} %compare_and_fusion) | copy-start | bytes 196
  158.1 11.2 %all-to-all-start.5 = ((f32[16,4,4,128]{3,2,1,0:T(4,128)}), f32[16,4,4,128]{3,2,1,0:T(4,128)S(1)}, u32[]{:S(2)}, u32[]{:S(2)}) async-start(f32[16,4,4,128]{3,2,1,0:T(4,128)} %bitcast.40), calls=%async_computation.5 | async-start | bytes 262144 | tf_op jit(solution)/shard_map/all_to_all | solution.py:154
  169.3 11.4 %all-to-all-start.7 = ((f32[16,4,4,128]{3,2,1,0:T(4,128)}), f32[16,4,4,128]{3,2,1,0:T(4,128)S(1)}, u32[]{:S(2)}, u32[]{:S(2)}) async-start(f32[16,4,4,128]{3,2,1,0:T(4,128)} %bitcast.46), calls=%async_computation.7 | async-start | bytes 262144 | tf_op jit(solution)/shard_map/all_to_all | solution.py:155
  180.7 99.6 %all-to-all-start.6 = ((f32[16,4,4,32,128]{4,3,2,1,0:T(8,128)}), f32[16,4,4,32,128]{4,3,2,1,0:T(8,128)}, u32[]{:S(2)}, u32[]{:S(2)}) async-start(f32[16,4,4,32,128]{4,3,2,1,0:T(8,128)} %select_select_fusion), calls=%async_computation.6 | async-start | bytes 8388608 | tf_op jit(solution)/shard_map/all_to_all | solution.py:153
  294.2 1.0 copy-start.2
  294.2 1.0 copy-start.7
Sparse Core Ops, SparseCore 0:
  8.9 22.2 all-gather.1
